TPU v7x, 32 devices: a whole 2x2x4 slice. The times are simulated.
32 devices in a mesh: parts: 2 (over y), rows: 4 (over x, core), cols: 4 (over z).
Axes of the slice: x: 2, y: 2, z: 4, core: 2. Of those that a mesh axis runs over, the one named last changes fastest.
Arguments:
- singles: bfloat16 [1024, 384], P(('parts', 'rows', 'cols')), parts along dimension 0, may hold values from -120 to 120
- pair: bfloat16 [1024, 512, 128], P(('parts', 'rows'), 'cols'), parts along dimension 0, may hold values from -6 to 6
- chain_sizes: int32 [16], P('parts'), parts along dimension 0, may hold values from 1 to 128, 512 in all
- single_proj: bfloat16 [384, 1536], replicated, may hold values from -1 to 1
- query_bias: float32 [384], replicated, may hold values from -5 to 5
- pair_proj: bfloat16 [128, 16], replicated, may hold values from -0.5 to 0.5
- out_proj: bfloat16 [384, 384], replicated, may hold values from -1.25 to 1.25
Outputs:
- update: bfloat16 [1024, 384], P(('parts', 'rows', 'cols')), parts along dimension 0
There are 2 independent parts, one for each index of `parts`. A program takes and returns all parts, laid end to end along the dimension named above; an argument that names none is the same for every part. Nothing has to cross between parts.
Inputs may be any that keep to these rules, and one draw needn't show every extreme that they name: `chain_sizes`: the first 7 entries count the tokens of the chains in order; the last one counts the padding tokens at the end of the complex.
All inputs are finite; a program needn't handle non-finite values.
Results may differ from a plain program's by a relative error of at most 0.004.
The roundings to bfloat16 on the way count: a program that leaves them out, or rounds other values in their place, can miss the bound.
Values may be sent and summed in bfloat16 or wider, within the bound.
A program may use at most 64 MiB of HBM per device.

v0:
```python
import math
import jax
import jax.numpy as jnp
from jax import lax
from jax.sharding import PartitionSpec as P


def normalize(matrix):
    average = jnp.mean(matrix, axis=-1, keepdims=True)
    centered = matrix - average
    variance = jnp.mean(centered * centered, axis=-1, keepdims=True)
    return centered * lax.rsqrt(variance + 1e-05)


def tile_bias(pair, pair_proj):
    tile_rows, tile_cols, channels = pair.shape
    head_count = pair_proj.shape[1]
    row_block = math.gcd(tile_rows, 32)
    blocks = pair.reshape(tile_rows // row_block, row_block, tile_cols, channels)

    def project(pair_rows):
        pair_normed = normalize(pair_rows.astype(jnp.float32)).astype(jnp.bfloat16)
        return jnp.einsum(
            "ikc,ch->hik", pair_normed, pair_proj, preferred_element_type=jnp.float32
        ).astype(jnp.bfloat16)

    stacked = lax.map(project, blocks)
    return jnp.moveaxis(stacked, 1, 0).reshape(head_count, tile_rows, tile_cols)


def shards(singles, pair, chain_sizes, single_proj, query_bias, pair_proj, out_proj):
    own_rows, features = singles.shape
    head_count = pair_proj.shape[1]
    head_dim = features // head_count
    score_scale = head_dim ** (-0.5)
    normed = normalize(singles.astype(jnp.float32)).astype(jnp.bfloat16)
    projected = jnp.dot(normed, single_proj, preferred_element_type=jnp.float32)
    queries = (projected[:, :features] + query_bias).astype(jnp.bfloat16)
    key_rows = projected[:, features : 2 * features].astype(jnp.bfloat16)
    values = projected[:, 2 * features : 3 * features].astype(jnp.bfloat16)
    gating = jax.nn.sigmoid(projected[:, 3 * features :])
    live_count = jnp.sum(chain_sizes[:-1])
    bias_tile = tile_bias(pair, pair_proj)
    key_value = jnp.concatenate([key_rows, values], axis=1)
    gathered = lax.all_gather(key_value, ("rows", "cols"), axis=0, tiled=True)
    bias_own = lax.all_to_all(bias_tile, "cols", split_axis=1, concat_axis=2, tiled=True)
    key_count = gathered.shape[0]
    key_heads = gathered[:, :features].reshape(key_count, head_count, head_dim)
    value_heads = gathered[:, features:].reshape(key_count, head_count, head_dim)
    query_heads = queries.reshape(own_rows, head_count, head_dim)
    scores = jnp.einsum(
        "qhd,khd->hqk", query_heads, key_heads, preferred_element_type=jnp.float32
    ) * score_scale + bias_own.astype(jnp.float32)
    key_live = jnp.arange(key_count, dtype=jnp.int32) < live_count
    scores = jnp.where(key_live[None, None, :], scores, -1e30)
    maxima = jnp.max(scores, axis=-1, keepdims=True)
    weights = jnp.exp(scores - maxima)
    totals = jnp.sum(weights, axis=-1)
    numerator = jnp.einsum(
        "hqk,khd->qhd",
        weights.astype(jnp.bfloat16),
        value_heads,
        preferred_element_type=jnp.float32,
    )
    averaged = (numerator / jnp.transpose(totals)[:, :, None]).reshape(own_rows, features)
    attended = (gating * averaged).astype(jnp.bfloat16)
    return jnp.dot(attended, out_proj, preferred_element_type=jnp.float32).astype(jnp.bfloat16)


def solution(mesh):
    placed = (
        P(("parts", "rows", "cols"), None),
        P(("parts", "rows"), "cols", None),
        P("parts"),
        P(),
        P(),
        P(),
        P(),
    )
    return jax.shard_map(
        shards,
        mesh=mesh,
        in_specs=placed,
        out_specs=P(("parts", "rows", "cols"), None),
        check_vma=False,
    )
```

profile of v0, /device:TPU:0, one launch (start us, length us, event | category | flops | bytes accessed | tf_op | source)
XLA Modules:
  0.0 86.1 jit_solution(3081833499026486826)
XLA Ops:
  0.0 28.6 %while.10 = (s32[]{:T(128)}, bf16[4,16,32,128]{3,1,2,0:T(8,128)(2,1)}, bf16[4,32,128,128]{3,2,1,0:T(8,128)(2,1)}, bf16[128,16]{0,1:T(8,128)(2,1)}, s32[]{:T(128)}) while((s32[]{:T(128)}, bf16[4,16,32,128]{3,1,2,0:T(8,128)(2,1)}, bf16[4,32,128,128]{3,2,1,0:T(8,128)(2,1)}, bf16[128,16]{0,1:T(8,128)(2,1)}, s32[]{:T(128)}) %tuple.23), condition=%wide.region_6.7_spmd, body=%wide.region_3.6_spmd.sunk | while | flops 22089728 | bytes 3445865 | solution.py:27
  0.0 1.7 %convert_reduce_fusion.3 = f32[32,128]{1,0:T(8,128)S(1)} fusion(bf16[4,32,128,128]{3,2,1,0:T(8,128)(2,1)} %get-tuple-element.77, s32[]{:T(128)S(6)} %copy.31), kind=kLoop, calls=%fused_computation.clone.1 | loop fusion | flops 1044480 | bytes 1064964 | tf_op jit(solution)/shard_map/while/body/eval_jaxpr/reduce_sum | solution.py:9
  1.7 2.3 %fusion.50 = f32[32,128]{1,0:T(8,128)S(1)} fusion(f32[32,128]{1,0:T(8,128)S(1)} %broadcast_multiply_fusion.3, bf16[4,32,128,128]{3,2,1,0:T(8,128)(2,1)} %get-tuple-element.77, s32[]{:T(128)S(6)} %copy.31), kind=kLoop, calls=%fused_computation.5.clone.1 | loop fusion | flops 2093056 | bytes 1081348 | tf_op jit(solution)/shard_map/while/body/eval_jaxpr/reduce_sum | solution.py:11
  4.1 3.1 %fusion.51 = bf16[4,16,32,128]{3,1,2,0:T(8,128)(2,1)} fusion(bf16[4,16,32,128]{3,1,2,0:T(8,128)(2,1)} %get-tuple-element.71, s32[]{:T(128)S(6)} %copy.31, f32[32,128]{1,0:T(8,128)S(1)} %add_rsqrt_fusion.3, f32[32,128]{1,0:T(8,128)S(1)} %broadcast_multiply_fusion.3, bf16[4,32,128,128]{3,2,1,0:T(8,128)(2,1)} %get-tuple-element.77, ...), kind=kOutput, calls=%fused_computation.9.clone.1 | convolution fusion | flops 18939904 | bytes 1217536 | tf_op jit(solution)/shard_map/while/body/eval_jaxpr/ikc,ch->hik/dot_general | solution.py:23
  7.2 1.6 %convert_reduce_fusion.3 = f32[32,128]{1,0:T(8,128)S(1)} fusion(bf16[4,32,128,128]{3,2,1,0:T(8,128)(2,1)} %get-tuple-element.77, s32[]{:T(128)S(6)} %copy.31), kind=kLoop, calls=%fused_computation.clone.1 | loop fusion | flops 1044480 | bytes 1064964 | tf_op jit(solution)/shard_map/while/body/eval_jaxpr/reduce_sum | solution.py:9
  8.8 2.3 %fusion.50 = f32[32,128]{1,0:T(8,128)S(1)} fusion(f32[32,128]{1,0:T(8,128)S(1)} %broadcast_multiply_fusion.3, bf16[4,32,128,128]{3,2,1,0:T(8,128)(2,1)} %get-tuple-element.77, s32[]{:T(128)S(6)} %copy.31), kind=kLoop, calls=%fused_computation.5.clone.1 | loop fusion | flops 2093056 | bytes 1081348 | tf_op jit(solution)/shard_map/while/body/eval_jaxpr/reduce_sum | solution.py:11
  11.2 3.2 %fusion.51 = bf16[4,16,32,128]{3,1,2,0:T(8,128)(2,1)} fusion(bf16[4,16,32,128]{3,1,2,0:T(8,128)(2,1)} %get-tuple-element.71, s32[]{:T(128)S(6)} %copy.31, f32[32,128]{1,0:T(8,128)S(1)} %add_rsqrt_fusion.3, f32[32,128]{1,0:T(8,128)S(1)} %broadcast_multiply_fusion.3, bf16[4,32,128,128]{3,2,1,0:T(8,128)(2,1)} %get-tuple-element.77, ...), kind=kOutput, calls=%fused_computation.9.clone.1 | convolution fusion | flops 18939904 | bytes 1217536 | tf_op jit(solution)/shard_map/while/body/eval_jaxpr/ikc,ch->hik/dot_general | solution.py:23
  14.4 1.6 %convert_reduce_fusion.3 = f32[32,128]{1,0:T(8,128)S(1)} fusion(bf16[4,32,128,128]{3,2,1,0:T(8,128)(2,1)} %get-tuple-element.77, s32[]{:T(128)S(6)} %copy.31), kind=kLoop, calls=%fused_computation.clone.1 | loop fusion | flops 1044480 | bytes 1064964 | tf_op jit(solution)/shard_map/while/body/eval_jaxpr/reduce_sum | solution.py:9
  16.0 2.3 %fusion.50 = f32[32,128]{1,0:T(8,128)S(1)} fusion(f32[32,128]{1,0:T(8,128)S(1)} %broadcast_multiply_fusion.3, bf16[4,32,128,128]{3,2,1,0:T(8,128)(2,1)} %get-tuple-element.77, s32[]{:T(128)S(6)} %copy.31), kind=kLoop, calls=%fused_computation.5.clone.1 | loop fusion | flops 2093056 | bytes 1081348 | tf_op jit(solution)/shard_map/while/body/eval_jaxpr/reduce_sum | solution.py:11
  18.3 3.2 %fusion.51 = bf16[4,16,32,128]{3,1,2,0:T(8,128)(2,1)} fusion(bf16[4,16,32,128]{3,1,2,0:T(8,128)(2,1)} %get-tuple-element.71, s32[]{:T(128)S(6)} %copy.31, f32[32,128]{1,0:T(8,128)S(1)} %add_rsqrt_fusion.3, f32[32,128]{1,0:T(8,128)S(1)} %broadcast_multiply_fusion.3, bf16[4,32,128,128]{3,2,1,0:T(8,128)(2,1)} %get-tuple-element.77, ...), kind=kOutput, calls=%fused_computation.9.clone.1 | convolution fusion | flops 18939904 | bytes 1217536 | tf_op jit(solution)/shard_map/while/body/eval_jaxpr/ikc,ch->hik/dot_general | solution.py:23
  21.5 1.6 %convert_reduce_fusion.3 = f32[32,128]{1,0:T(8,128)S(1)} fusion(bf16[4,32,128,128]{3,2,1,0:T(8,128)(2,1)} %get-tuple-element.77, s32[]{:T(128)S(6)} %copy.31), kind=kLoop, calls=%fused_computation.clone.1 | loop fusion | flops 1044480 | bytes 1064964 | tf_op jit(solution)/shard_map/while/body/eval_jaxpr/reduce_sum | solution.py:9
  23.1 2.3 %fusion.50 = f32[32,128]{1,0:T(8,128)S(1)} fusion(f32[32,128]{1,0:T(8,128)S(1)} %broadcast_multiply_fusion.3, bf16[4,32,128,128]{3,2,1,0:T(8,128)(2,1)} %get-tuple-element.77, s32[]{:T(128)S(6)} %copy.31), kind=kLoop, calls=%fused_computation.5.clone.1 | loop fusion | flops 2093056 | bytes 1081348 | tf_op jit(solution)/shard_map/while/body/eval_jaxpr/reduce_sum | solution.py:11
  25.5 3.2 %fusion.51 = bf16[4,16,32,128]{3,1,2,0:T(8,128)(2,1)} fusion(bf16[4,16,32,128]{3,1,2,0:T(8,128)(2,1)} %get-tuple-element.71, s32[]{:T(128)S(6)} %copy.31, f32[32,128]{1,0:T(8,128)S(1)} %add_rsqrt_fusion.3, f32[32,128]{1,0:T(8,128)S(1)} %broadcast_multiply_fusion.3, bf16[4,32,128,128]{3,2,1,0:T(8,128)(2,1)} %get-tuple-element.77, ...), kind=kOutput, calls=%fused_computation.9.clone.1 | convolution fusion | flops 18939904 | bytes 1217536 | tf_op jit(solution)/shard_map/while/body/eval_jaxpr/ikc,ch->hik/dot_general | solution.py:23
  28.6 6.5 %all-to-all-start = ((bf16[16,128,128]{2,0,1:T(8,128)(2,1)}), bf16[16,128,128]{2,0,1:T(8,128)(2,1)S(1)}, u32[]{:S(2)}, u32[]{:S(2)}) async-start(bf16[16,128,128]{2,0,1:T(8,128)(2,1)} %bitcast.9), calls=%async_computation | async-start | bytes 1048576 | tf_op jit(solution)/shard_map/all_to_all | solution.py:46
  35.1 0.1 convert_reduce_fusion.1
  35.2 0.2 fusion.22
  35.4 0.4 fusion.31
  35.8 0.0 copy-start.5
  35.8 0.1 copy.24
  36.0 46.1 %all_gather.3 = bf16[512,768]{1,0:T(8,128)(2,1)S(1)} all-gather(bf16[32,768]{1,0:T(8,128)(2,1)S(1)} %slice.53), channel_id=1, replica_groups=mesh['parts'=2,'rows'=4,'cols'=4] {'rows','cols'}, dimensions={0}, use_global_device_ids=true | all-gather | bytes 835584 | tf_op jit(solution)/shard_map/all_gather | solution.py:45
  82.1 0.1 fusion.37
  82.2 0.2 copy.19
  82.4 0.2 copy.18
  82.6 0.6 slice_reduce_fusion
  83.2 0.6 iota_compare_fusion
  83.9 0.1 copy.21
  84.0 0.0 copy-start.1
  84.0 0.5 fusion.38
  84.5 0.3 fusion.16
  84.8 0.3 fusion.15
  85.2 0.1 copy.25
  85.3 0.8 convolution_convert_fusion.1
  (30 shorter events, 0.1 us)
Async XLA Ops:
  0.0 35.4 %copy-start = (bf16[384,1536]{1,0:T(8,128)(2,1)S(1)}, bf16[384,1536]{1,0:T(8,128)(2,1)}, u32[]{:S(2)}) copy-start(bf16[384,1536]{1,0:T(8,128)(2,1)} %param.12) | copy-start | bytes 3538948
  0.0 35.1 %copy-start.2 = (bf16[32,384]{1,0:T(8,128)(2,1)S(1)}, bf16[32,384]{1,0:T(8,128)(2,1)}, u32[]{:S(2)}) copy-start(bf16[32,384]{1,0:T(8,128)(2,1)} %param.9) | copy-start | bytes 73732
  0.0 4.1 %copy-start.4 = (bf16[128,16]{0,1:T(8,128)(2,1)S(1)}, bf16[128,16]{0,1:T(8,128)(2,1)}, u32[]{:S(2)}) copy-start(bf16[128,16]{0,1:T(8,128)(2,1)} %get-tuple-element.78) | copy-start | bytes 12292 | tf_op jit(solution)/shard_map/while
  7.2 4.0 %copy-start.4 = (bf16[128,16]{0,1:T(8,128)(2,1)S(1)}, bf16[128,16]{0,1:T(8,128)(2,1)}, u32[]{:S(2)}) copy-start(bf16[128,16]{0,1:T(8,128)(2,1)} %get-tuple-element.78) | copy-start | bytes 12292 | tf_op jit(solution)/shard_map/while
  14.4 4.0 %copy-start.4 = (bf16[128,16]{0,1:T(8,128)(2,1)S(1)}, bf16[128,16]{0,1:T(8,128)(2,1)}, u32[]{:S(2)}) copy-start(bf16[128,16]{0,1:T(8,128)(2,1)} %get-tuple-element.78) | copy-start | bytes 12292 | tf_op jit(solution)/shard_map/while
  21.5 4.0 %copy-start.4 = (bf16[128,16]{0,1:T(8,128)(2,1)S(1)}, bf16[128,16]{0,1:T(8,128)(2,1)}, u32[]{:S(2)}) copy-start(bf16[128,16]{0,1:T(8,128)(2,1)} %get-tuple-element.78) | copy-start | bytes 12292 | tf_op jit(solution)/shard_map/while
  28.6 7.2 %copy-start.3 = (f32[384]{0:T(512)S(1)}, f32[384]{0:T(512)}, u32[]{:S(2)}) copy-start(f32[384]{0:T(512)} %param.13) | copy-start | bytes 4612
  28.6 55.3 %all-to-all-start = ((bf16[16,128,128]{2,0,1:T(8,128)(2,1)}), bf16[16,128,128]{2,0,1:T(8,128)(2,1)S(1)}, u32[]{:S(2)}, u32[]{:S(2)}) async-start(bf16[16,128,128]{2,0,1:T(8,128)(2,1)} %bitcast.9), calls=%async_computation | async-start | bytes 1048576 | tf_op jit(solution)/shard_map/all_to_all | solution.py:46
  35.8 46.8 %copy-start.5 = (s32[8]{0:T(128)S(1)}, s32[8]{0:T(128)}, u32[]{:S(2)}) copy-start(s32[8]{0:T(128)} %param.11) | copy-start | bytes 100
  84.0 1.3 %copy-start.1 = (bf16[384,384]{1,0:T(8,128)(2,1)S(1)}, bf16[384,384]{1,0:T(8,128)(2,1)}, u32[]{:S(2)}) copy-start(bf16[384,384]{1,0:T(8,128)(2,1)} %param.15) | copy-start | bytes 884740
where the time goes:
time: 86.6 us; the launch traced here: 86.1 us
  blocking collectives  46.1 us (53%)
  other arithmetic  17.8 us (21%)
  matrix products  14.6 us (17%)
  starting transfers between devices  6.48 us (7%)
  local copies, waits for them, and re-layouts  0.87 us (1%)
    all_gather x1, blocking collectives, shards(): gathered = lax.all_gather(key_value, ('rows', 'cols'), axis=0, tiled=True)  46.1 us
    dot_general x4, matrix products, project(): jnp.einsum('ikc,ch->hik', pair_normed, pair_proj, preferred_element_type=...  12.6 us
    reduce_sum x5, other arithmetic, normalize(): variance = jnp.mean(centered * centered, axis=-1, keepdims=True)  9.52 us
    reduce_sum x5, other arithmetic, normalize(): average = jnp.mean(matrix, axis=-1, keepdims=True)  6.56 us
    all_to_all x1, starting transfers between devices, shards(): lax.all_to_all(bias_tile, 'cols', split_axis=1, concat_axis=2, tiled=True)  6.48 us
  transfers between devices with their start and end apart: 1, of which 0 were waited for; matrix products, arithmetic and copies ran while one was open for 3% of the time, Pallas kernels for 0%

commit v1 on v0

--- a/solution.py
+++ b/solution.py
@@ -3,6 +3,22 @@
 import jax.numpy as jnp
 from jax import lax
 from jax.sharding import PartitionSpec as P
+
+
+def swapped_with_each(x, axis, split, join):
+    ways, here = (lax.axis_size(axis), lax.axis_index(axis))
+    width = x.shape[split] // ways
+    shape = list(x.shape)
+    shape[split] = width
+    height = shape[join]
+    shape[join] = height * ways
+    full = jnp.zeros(shape, x.dtype)
+    for mask in range(ways):
+        part = lax.dynamic_slice_in_dim(x, (here ^ mask) * width, width, axis=split)
+        if mask:
+            part = lax.ppermute(part, axis, [(d, d ^ mask) for d in range(ways)])
+        full = lax.dynamic_update_slice_in_dim(full, part, (here ^ mask) * height, axis=join)
+    return full
 
 
 def normalize(matrix):
@@ -43,7 +59,7 @@
     bias_tile = tile_bias(pair, pair_proj)
     key_value = jnp.concatenate([key_rows, values], axis=1)
     gathered = lax.all_gather(key_value, ("rows", "cols"), axis=0, tiled=True)
-    bias_own = lax.all_to_all(bias_tile, "cols", split_axis=1, concat_axis=2, tiled=True)
+    bias_own = swapped_with_each(bias_tile, "cols", 1, 2)
     key_count = gathered.shape[0]
     key_heads = gathered[:, :features].reshape(key_count, head_count, head_dim)
     value_heads = gathered[:, features:].reshape(key_count, head_count, head_dim)

time: 86.6 us -> 81.5 us (0.941)
  blocking collectives: 46.1 us -> 42.4 us
  matrix products: 14.6 us -> 12 us
  local copies, waits for them, and re-layouts: 0.87 us -> 2.71 us
    all_to_all x1 -> x0, starting transfers between devices: 6.48 us -> none  [shards(): lax.all_to_all(bias_tile, 'cols', split_axis=1, concat_axis=2, tiled=True)]
    ppermute x0 -> x3, starting transfers between devices: none -> 5.64 us  [swapped_with_each(): part = lax.ppermute(part, axis, [(d, d ^ mask) for d in range(ways)])]
    all_gather x1, blocking collectives: 46.1 us -> 42.4 us  [shards(): gathered = lax.all_gather(key_value, ('rows', 'cols'), axis=0, tiled=True)]
    dot_general x4, matrix products: 12.6 us -> 10.1 us  [project(): jnp.einsum('ikc,ch->hik', pair_normed, pair_proj, preferred_element_type=...]
    dynamic_update_slice x0 -> x3, local copies, waits for them, and re-layouts: none -> 1.02 us  [swapped_with_each(): lax.dynamic_update_slice_in_dim(full, part, (here ^ mask) * height, axis=...]
  transfers between devices with their start and end apart: 1 -> 3, of which waited for: 0 -> 0; matrix products, arithmetic and copies ran while one was open for 3% -> 4% of each run, Pallas kernels for 0% -> 0%
where the time goes in v1:
time: 81.5 us; the launch traced here: 81 us
  blocking collectives  42.4 us (52%)
  other arithmetic  17.7 us (22%)
  matrix products  12 us (15%)
  starting transfers between devices  5.64 us (7%)
  local copies, waits for them, and re-layouts  2.71 us (3%)
    all_gather x1, blocking collectives, shards(): gathered = lax.all_gather(key_value, ('rows', 'cols'), axis=0, tiled=True)  42.4 us
    dot_general x4, matrix products, project(): jnp.einsum('ikc,ch->hik', pair_normed, pair_proj, preferred_element_type=...  10.1 us
    reduce_sum x5, other arithmetic, normalize(): variance = jnp.mean(centered * centered, axis=-1, keepdims=True)  9.52 us
    reduce_sum x5, other arithmetic, normalize(): average = jnp.mean(matrix, axis=-1, keepdims=True)  6.53 us
    ppermute x3, starting transfers between devices, swapped_with_each(): part = lax.ppermute(part, axis, [(d, d ^ mask) for d in range(ways)])  5.64 us
  transfers between devices with their start and end apart: 3, of which 0 were waited for; matrix products, arithmetic and copies ran while one was open for 4% of the time, Pallas kernels for 0%

profile of v1, /device:TPU:0, one launch (start us, length us, event | category | flops | bytes accessed | tf_op | source)
XLA Modules:
  0.0 81.0 jit_solution(13715690555928553561)
XLA Ops:
  0.0 26.1 %while.10 = (s32[]{:T(128)}, bf16[4,16,32,128]{3,1,2,0:T(8,128)(2,1)S(1)}, bf16[4,32,128,128]{3,2,1,0:T(8,128)(2,1)}, bf16[128,16]{0,1:T(8,128)(2,1)}, s32[]{:T(128)}) while((s32[]{:T(128)}, bf16[4,16,32,128]{3,1,2,0:T(8,128)(2,1)S(1)}, bf16[4,32,128,128]{3,2,1,0:T(8,128)(2,1)}, bf16[128,16]{0,1:T(8,128)(2,1)}, s32[]{:T(128)}) %tuple.26), condition=%wide.region_6.7_spmd, body=%wide.region_3.6_spmd.sunk | while | flops 22089728 | bytes 3445865 | solution.py:43
  0.0 1.7 %convert_reduce_fusion.3 = f32[32,128]{1,0:T(8,128)S(1)} fusion(bf16[4,32,128,128]{3,2,1,0:T(8,128)(2,1)} %get-tuple-element.81, s32[]{:T(128)S(6)} %copy.23), kind=kLoop, calls=%fused_computation.clone.1 | loop fusion | flops 1044480 | bytes 1064964 | tf_op jit(solution)/shard_map/while/body/eval_jaxpr/reduce_sum | solution.py:25
  1.7 2.3 %fusion.48 = f32[32,128]{1,0:T(8,128)S(1)} fusion(f32[32,128]{1,0:T(8,128)S(1)} %broadcast_multiply_fusion.3, bf16[4,32,128,128]{3,2,1,0:T(8,128)(2,1)} %get-tuple-element.81, s32[]{:T(128)S(6)} %copy.23), kind=kLoop, calls=%fused_computation.5.clone.1 | loop fusion | flops 2093056 | bytes 1081348 | tf_op jit(solution)/shard_map/while/body/eval_jaxpr/reduce_sum | solution.py:27
  4.1 2.5 %fusion.49 = bf16[4,16,32,128]{3,1,2,0:T(8,128)(2,1)S(1)} fusion(bf16[4,16,32,128]{3,1,2,0:T(8,128)(2,1)S(1)} %get-tuple-element.75, s32[]{:T(128)S(6)} %copy.23, f32[32,128]{1,0:T(8,128)S(1)} %add_rsqrt_fusion.3, f32[32,128]{1,0:T(8,128)S(1)} %broadcast_multiply_fusion.3, bf16[4,32,128,128]{3,2,1,0:T(8,128)(2,1)} %get-tuple-element.81, ...), kind=kOutput, calls=%fused_computation.9.clone.1 | convolution fusion | flops 18939904 | bytes 1217536 | tf_op jit(solution)/shard_map/while/body/eval_jaxpr/ikc,ch->hik/dot_general | solution.py:39
  6.6 1.6 %convert_reduce_fusion.3 = f32[32,128]{1,0:T(8,128)S(1)} fusion(bf16[4,32,128,128]{3,2,1,0:T(8,128)(2,1)} %get-tuple-element.81, s32[]{:T(128)S(6)} %copy.23), kind=kLoop, calls=%fused_computation.clone.1 | loop fusion | flops 1044480 | bytes 1064964 | tf_op jit(solution)/shard_map/while/body/eval_jaxpr/reduce_sum | solution.py:25
  8.2 2.3 %fusion.48 = f32[32,128]{1,0:T(8,128)S(1)} fusion(f32[32,128]{1,0:T(8,128)S(1)} %broadcast_multiply_fusion.3, bf16[4,32,128,128]{3,2,1,0:T(8,128)(2,1)} %get-tuple-element.81, s32[]{:T(128)S(6)} %copy.23), kind=kLoop, calls=%fused_computation.5.clone.1 | loop fusion | flops 2093056 | bytes 1081348 | tf_op jit(solution)/shard_map/while/body/eval_jaxpr/reduce_sum | solution.py:27
  10.6 2.5 %fusion.49 = bf16[4,16,32,128]{3,1,2,0:T(8,128)(2,1)S(1)} fusion(bf16[4,16,32,128]{3,1,2,0:T(8,128)(2,1)S(1)} %get-tuple-element.75, s32[]{:T(128)S(6)} %copy.23, f32[32,128]{1,0:T(8,128)S(1)} %add_rsqrt_fusion.3, f32[32,128]{1,0:T(8,128)S(1)} %broadcast_multiply_fusion.3, bf16[4,32,128,128]{3,2,1,0:T(8,128)(2,1)} %get-tuple-element.81, ...), kind=kOutput, calls=%fused_computation.9.clone.1 | convolution fusion | flops 18939904 | bytes 1217536 | tf_op jit(solution)/shard_map/while/body/eval_jaxpr/ikc,ch->hik/dot_general | solution.py:39
  13.1 1.6 %convert_reduce_fusion.3 = f32[32,128]{1,0:T(8,128)S(1)} fusion(bf16[4,32,128,128]{3,2,1,0:T(8,128)(2,1)} %get-tuple-element.81, s32[]{:T(128)S(6)} %copy.23), kind=kLoop, calls=%fused_computation.clone.1 | loop fusion | flops 1044480 | bytes 1064964 | tf_op jit(solution)/shard_map/while/body/eval_jaxpr/reduce_sum | solution.py:25
  14.7 2.3 %fusion.48 = f32[32,128]{1,0:T(8,128)S(1)} fusion(f32[32,128]{1,0:T(8,128)S(1)} %broadcast_multiply_fusion.3, bf16[4,32,128,128]{3,2,1,0:T(8,128)(2,1)} %get-tuple-element.81, s32[]{:T(128)S(6)} %copy.23), kind=kLoop, calls=%fused_computation.5.clone.1 | loop fusion | flops 2093056 | bytes 1081348 | tf_op jit(solution)/shard_map/while/body/eval_jaxpr/reduce_sum | solution.py:27
  17.1 2.5 %fusion.49 = bf16[4,16,32,128]{3,1,2,0:T(8,128)(2,1)S(1)} fusion(bf16[4,16,32,128]{3,1,2,0:T(8,128)(2,1)S(1)} %get-tuple-element.75, s32[]{:T(128)S(6)} %copy.23, f32[32,128]{1,0:T(8,128)S(1)} %add_rsqrt_fusion.3, f32[32,128]{1,0:T(8,128)S(1)} %broadcast_multiply_fusion.3, bf16[4,32,128,128]{3,2,1,0:T(8,128)(2,1)} %get-tuple-element.81, ...), kind=kOutput, calls=%fused_computation.9.clone.1 | convolution fusion | flops 18939904 | bytes 1217536 | tf_op jit(solution)/shard_map/while/body/eval_jaxpr/ikc,ch->hik/dot_general | solution.py:39
  19.7 1.6 %convert_reduce_fusion.3 = f32[32,128]{1,0:T(8,128)S(1)} fusion(bf16[4,32,128,128]{3,2,1,0:T(8,128)(2,1)} %get-tuple-element.81, s32[]{:T(128)S(6)} %copy.23), kind=kLoop, calls=%fused_computation.clone.1 | loop fusion | flops 1044480 | bytes 1064964 | tf_op jit(solution)/shard_map/while/body/eval_jaxpr/reduce_sum | solution.py:25
  21.2 2.3 %fusion.48 = f32[32,128]{1,0:T(8,128)S(1)} fusion(f32[32,128]{1,0:T(8,128)S(1)} %broadcast_multiply_fusion.3, bf16[4,32,128,128]{3,2,1,0:T(8,128)(2,1)} %get-tuple-element.81, s32[]{:T(128)S(6)} %copy.23), kind=kLoop, calls=%fused_computation.5.clone.1 | loop fusion | flops 2093056 | bytes 1081348 | tf_op jit(solution)/shard_map/while/body/eval_jaxpr/reduce_sum | solution.py:27
  23.6 2.5 %fusion.49 = bf16[4,16,32,128]{3,1,2,0:T(8,128)(2,1)S(1)} fusion(bf16[4,16,32,128]{3,1,2,0:T(8,128)(2,1)S(1)} %get-tuple-element.75, s32[]{:T(128)S(6)} %copy.23, f32[32,128]{1,0:T(8,128)S(1)} %add_rsqrt_fusion.3, f32[32,128]{1,0:T(8,128)S(1)} %broadcast_multiply_fusion.3, bf16[4,32,128,128]{3,2,1,0:T(8,128)(2,1)} %get-tuple-element.81, ...), kind=kOutput, calls=%fused_computation.9.clone.1 | convolution fusion | flops 18939904 | bytes 1217536 | tf_op jit(solution)/shard_map/while/body/eval_jaxpr/ikc,ch->hik/dot_general | solution.py:39
  26.2 0.1 copy.16
  26.4 0.8 constant_dynamic-slice_fusion
  27.2 5.1 %collective-permute-start.2 = (bf16[16,32,128]{2,1,0:T(8,128)(2,1)}, bf16[16,32,128]{2,1,0:T(8,128)(2,1)S(1)}, u32[]{:S(2)}, u32[]{:S(2)}) collective-permute-start(bf16[16,32,128]{2,1,0:T(8,128)(2,1)} %get-tuple-element.38), channel_id=1, source_target_pairs={{0,3},{1,2},{2,1},{3,0},{4,7},{5,6},{6,5},{7,4},{8,11},{9,10},{10,... | collective-permute-start | bytes 393224 | tf_op jit(solution)/shard_map/ppermute | solution.py:19
  32.2 0.6 collective-permute-start
  32.8 0.1 convert_reduce_fusion.1
  32.9 0.2 fusion.20
  33.1 0.4 fusion.29
  33.5 42.4 %all_gather.3 = bf16[512,768]{1,0:T(8,128)(2,1)S(1)} all-gather(bf16[32,768]{1,0:T(8,128)(2,1)S(1)} %slice.53), channel_id=1, replica_groups=mesh['parts'=2,'rows'=4,'cols'=4] {'rows','cols'}, dimensions={0}, use_global_device_ids=true | all-gather | bytes 835584 | tf_op jit(solution)/shard_map/all_gather | solution.py:61
  76.0 0.6 slice_reduce_fusion
  76.7 0.6 iota_compare_fusion
  77.4 0.1 copy.18
  77.5 0.2 copy.14
  77.7 0.2 copy.13
  77.9 0.9 %constant_dynamic-update-slice_fusion.1 = bf16[16,32,512]{2,1,0:T(8,128)(2,1)S(1)} fusion(bf16[16,32,512]{2,1,0:T(8,128)(2,1)S(1)} %get-tuple-element.41, bf16[16,32,128]{2,1,0:T(8,128)(2,1)} %collective-permute-done, s32[]{:T(128)S(6)} %select_n.31), kind=kLoop, calls=%fused_computation.49 | loop fusion | bytes 262148 | tf_op jit(solution)/shard_map/dynamic_update_slice | solution.py:20
  79.0 0.5 fusion.36
  79.4 0.3 fusion.14
  79.8 0.3 fusion.13
  80.1 0.1 copy.19
  80.2 0.8 convolution_convert_fusion.1
  (39 shorter events, 0.3 us)
Async XLA Ops:
  0.0 33.1 %copy-start = (bf16[384,1536]{1,0:T(8,128)(2,1)S(1)}, bf16[384,1536]{1,0:T(8,128)(2,1)}, u32[]{:S(2)}) copy-start(bf16[384,1536]{1,0:T(8,128)(2,1)} %param.12) | copy-start | bytes 3538948
  0.0 4.1 %copy-start.4 = (bf16[128,16]{0,1:T(8,128)(2,1)S(1)}, bf16[128,16]{0,1:T(8,128)(2,1)}, u32[]{:S(2)}) copy-start(bf16[128,16]{0,1:T(8,128)(2,1)} %get-tuple-element.82) | copy-start | bytes 12292 | tf_op jit(solution)/shard_map/while
  6.6 4.0 %copy-start.4 = (bf16[128,16]{0,1:T(8,128)(2,1)S(1)}, bf16[128,16]{0,1:T(8,128)(2,1)}, u32[]{:S(2)}) copy-start(bf16[128,16]{0,1:T(8,128)(2,1)} %get-tuple-element.82) | copy-start | bytes 12292 | tf_op jit(solution)/shard_map/while
  13.1 4.0 %copy-start.4 = (bf16[128,16]{0,1:T(8,128)(2,1)S(1)}, bf16[128,16]{0,1:T(8,128)(2,1)}, u32[]{:S(2)}) copy-start(bf16[128,16]{0,1:T(8,128)(2,1)} %get-tuple-element.82) | copy-start | bytes 12292 | tf_op jit(solution)/shard_map/while
  19.6 4.0 %copy-start.4 = (bf16[128,16]{0,1:T(8,128)(2,1)S(1)}, bf16[128,16]{0,1:T(8,128)(2,1)}, u32[]{:S(2)}) copy-start(bf16[128,16]{0,1:T(8,128)(2,1)} %get-tuple-element.82) | copy-start | bytes 12292 | tf_op jit(solution)/shard_map/while
  26.1 6.7 %copy-start.2 = (bf16[32,384]{1,0:T(8,128)(2,1)S(1)}, bf16[32,384]{1,0:T(8,128)(2,1)}, u32[]{:S(2)}) copy-start(bf16[32,384]{1,0:T(8,128)(2,1)} %param.9) | copy-start | bytes 73732
  26.2 7.3 %copy-start.3 = (f32[384]{0:T(512)S(1)}, f32[384]{0:T(512)}, u32[]{:S(2)}) copy-start(f32[384]{0:T(512)} %param.13) | copy-start | bytes 4612
  27.2 48.9 %copy-start.5 = (s32[8]{0:T(128)S(1)}, s32[8]{0:T(128)}, u32[]{:S(2)}) copy-start(s32[8]{0:T(128)} %param.11) | copy-start | bytes 100
  27.2 51.7 %collective-permute-start.2 = (bf16[16,32,128]{2,1,0:T(8,128)(2,1)}, bf16[16,32,128]{2,1,0:T(8,128)(2,1)S(1)}, u32[]{:S(2)}, u32[]{:S(2)}) collective-permute-start(bf16[16,32,128]{2,1,0:T(8,128)(2,1)} %get-tuple-element.38), channel_id=1, source_target_pairs={{0,3},{1,2},{2,1},{3,0},{4,7},{5,6},{6,5},{7,4},{8,11},{9,10},{10,... | collective-permute-start | bytes 393224 | tf_op jit(solution)/shard_map/ppermute | solution.py:19
  32.2 46.6 %collective-permute-start.1 = (bf16[16,32,128]{2,1,0:T(8,128)(2,1)}, bf16[16,32,128]{2,1,0:T(8,128)(2,1)S(1)}, u32[]{:S(2)}, u32[]{:S(2)}) collective-permute-start(bf16[16,32,128]{2,1,0:T(8,128)(2,1)} %get-tuple-element.39), channel_id=1, source_target_pairs={{0,2},{1,3},{2,0},{3,1},{4,6},{5,7},{6,4},{7,5},{8,10},{9,11},{10,... | collective-permute-start | bytes 393224 | tf_op jit(solution)/shard_map/ppermute | solution.py:19
  32.2 45.7 %collective-permute-start = (bf16[16,32,128]{2,1,0:T(8,128)(2,1)}, bf16[16,32,128]{2,1,0:T(8,128)(2,1)}, u32[]{:S(2)}, u32[]{:S(2)}) collective-permute-start(bf16[16,32,128]{2,1,0:T(8,128)(2,1)} %get-tuple-element.40), channel_id=1, source_target_pairs={{0,1},{1,0},{2,3},{3,2},{4,5},{5,4},{6,7},{7,6},{8,9},{9,8},{10,11... | collective-permute-start | bytes 393224 | tf_op jit(solution)/shard_map/ppermute | solution.py:19
  79.0 1.3 %copy-start.1 = (bf16[384,384]{1,0:T(8,128)(2,1)S(1)}, bf16[384,384]{1,0:T(8,128)(2,1)}, u32[]{:S(2)}) copy-start(bf16[384,384]{1,0:T(8,128)(2,1)} %param.15) | copy-start | bytes 884740
